TPU v7x, 32 devices: a whole 2x2x4 slice. The times are simulated.
32 devices in a mesh: rows: 8 (over y, x, core), grp: 4 (over z).
Axes of the slice: x: 2, y: 2, z: 4, core: 2. Of those that a mesh axis runs over, the one named last changes fastest.
Arguments:
- matrix: bfloat16 [16384, 2048], P(('rows', 'grp')), may hold values from -0.09375 to 0.09375
- right_side: bfloat16 [16384, 128], P(('rows', 'grp')), may hold values from -6 to 6
- precond: bfloat16 [2048, 2048], replicated, may hold values from -1 to 3
- row_counts: int32 [32], P(('rows', 'grp')), may hold values from 64 to 512, as said below
Outputs:
- solution: float32 [2048, 128], P(None, 'grp')
- coeffs: float32 [2048, 128], P(None, 'grp')
- rel_residual: float32 [128], P('grp')
Inputs may be any that keep to these rules, and one draw needn't show every extreme that they name: Device d holds A's rows in its first row_counts[d] slots of 512; some device is full in every draw.
All inputs are finite; a program needn't handle non-finite values.
Results may differ from a plain program's by a relative error of at most 0.0128.
Values may be sent and summed in bfloat16 or wider, within the bound.
A program may use at most 64 MiB of HBM per device.

v0:
```python
import jax
import jax.numpy as jnp
from jax import lax
from jax.sharding import PartitionSpec as P

ITERS = 3
floor_sq = 0.01


def pull_partial(matrix, residue):
    partial_value = lax.dot_general(
        matrix,
        residue.astype(jnp.bfloat16),
        (((0,), (0,)), ((), ())),
        preferred_element_type=jnp.float32,
    )
    squares = jnp.sum(residue * residue, axis=0, keepdims=True)
    return (partial_value, squares)


def column_section(precond, partial_value, squares, right_vec):
    u_norm = jnp.sqrt(squares + floor_sq)
    pulled = lax.dot_general(
        precond,
        (partial_value / u_norm).astype(jnp.bfloat16),
        (((0,), (0,)), ((), ())),
        preferred_element_type=jnp.float32,
    )
    raw_vec = pulled - u_norm * right_vec
    v_norm = jnp.sqrt(jnp.sum(raw_vec * raw_vec, axis=0, keepdims=True) + floor_sq)
    return (u_norm, raw_vec / v_norm, v_norm)


def shards(matrix, right_side, precond, row_counts):
    local_rows, width = matrix.shape
    count = row_counts[0]
    live_rows = (lax.broadcasted_iota(jnp.int32, (local_rows, 1), 0) < count).astype(jnp.float32)

    def row_pass(pushed, v_norm_all, left_vec):
        if pushed is None:
            residue = live_rows * right_side.astype(jnp.float32)
        else:
            residue = live_rows * (
                jnp.dot(matrix, pushed, preferred_element_type=jnp.float32) - v_norm_all * left_vec
            )
        partial_value, squares = pull_partial(matrix, residue)
        return (residue, partial_value, squares)

    def reduce_cols(partial_value, squares):
        shared, shared_sq = (
            lax.psum_scatter(partial_value, "grp", scatter_dimension=1, tiled=True),
            lax.psum_scatter(squares, "grp", scatter_dimension=1, tiled=True),
        )
        return lax.psum((shared, shared_sq), "rows")

    def share_cols(right_vec, v_norm, u_norm):
        pushed = jnp.dot(
            precond, right_vec.astype(jnp.bfloat16), preferred_element_type=jnp.float32
        ).astype(jnp.bfloat16)
        pushed = lax.all_gather(pushed, "grp", axis=1, tiled=True)
        norms = lax.all_gather(jnp.concatenate([v_norm, u_norm], axis=0), "grp", axis=1, tiled=True)
        return (pushed, norms[0:1], norms[1:2])

    residue, partial_value, squares = row_pass(None, None, None)
    partial_value, squares = reduce_cols(partial_value, squares)
    u_norm, right_vec, v_norm = column_section(
        precond, partial_value, squares, jnp.zeros((width, partial_value.shape[1]), jnp.float32)
    )
    phi_bar = u_norm
    rho_bar = v_norm
    search = right_vec
    coeffs = jnp.zeros(right_vec.shape, jnp.float32)
    start_norm = u_norm
    pushed, v_norm_all, u_norm_all = share_cols(right_vec, v_norm, u_norm)
    left_vec = residue / u_norm_all
    for turn_index in range(ITERS):
        residue, partial_value, squares = row_pass(pushed, v_norm_all, left_vec)
        partial_value, squares = reduce_cols(partial_value, squares)
        u_norm, next_vec, next_norm = column_section(precond, partial_value, squares, right_vec)
        radius = jnp.sqrt(rho_bar * rho_bar + u_norm * u_norm)
        cosine = rho_bar / radius
        sine_part = u_norm / radius
        coupling = sine_part * next_norm
        rho_bar = -cosine * next_norm
        phi_step = cosine * phi_bar
        phi_bar = sine_part * phi_bar
        coeffs = coeffs + phi_step / radius * search
        search = next_vec - coupling / radius * search
        right_vec = next_vec
        v_norm = next_norm
        if turn_index + 1 < ITERS:
            pushed, v_norm_all, u_norm_all = share_cols(right_vec, v_norm, u_norm)
            left_vec = residue / u_norm_all
    ratio = phi_bar / start_norm
    solution = jnp.dot(precond, coeffs.astype(jnp.bfloat16), preferred_element_type=jnp.float32)
    return (solution, coeffs, ratio[0])


def solution(mesh):
    return jax.shard_map(
        shards,
        mesh=mesh,
        in_specs=(P(("rows", "grp"), None), P(("rows", "grp"), None), P(), P(("rows", "grp"))),
        out_specs=(P(None, "grp"), P(None, "grp"), P("grp")),
        check_vma=False,
    )
```

profile of v0, /device:TPU:0, one launch (start us, length us, event | category | flops | bytes accessed | tf_op | source)
XLA Modules:
  0.0 477.1 jit_solution(473941250615389567)
XLA Ops:
  7.2 0.0 reduce-scatter.22.cloned.1.call-start
  8.0 1.0 copy.12
  9.0 0.1 multiply_reduce_fusion.5
  9.2 0.7 copy.16
  9.9 0.0 reduce-scatter.16.cloned.1.call-start
  10.0 1.4 convolution_bitcast_fusion.2
  11.4 0.0 reduce-scatter.16.cloned.1.call-update
  11.5 0.0 all-reduce.4.cloned.1.call-start
  11.5 21.3 %reduce-scatter.22.cloned.1.call-done = f32[32,1]{1,0:T(8,128)} async-done(((f32[128,1]{1,0:T(8,128)}), f32[32,1]{1,0:T(8,128)}) %reduce-scatter.22.cloned.1.call-update) | async-done | bytes 144
  32.8 0.8 copy.17
  33.6 11.8 %psum.50 = f32[1,32]{1,0:T(1,128)S(1)} all-reduce(f32[1,32]{1,0:T(1,128)S(1)} %copy.17), channel_id=1, replica_groups=mesh['rows'=8,'grp'=4] {'rows'}, use_global_device_ids=true, to_apply=%region_4.0 | all-reduce | flops 32 | bytes 256 | tf_op jit(solution)/shard_map/psum | solution.py:54
  45.5 15.1 %reduce-scatter.16.cloned.1.call-done = f32[2048,32]{0,1:T(8,128)} async-done(((f32[2048,128]{0,1:T(8,128)}), f32[2048,32]{0,1:T(8,128)}) %reduce-scatter.16.cloned.1.call-update) | async-done | bytes 262160 | tf_op jit(solution)/shard_map/reduce_scatter | solution.py:51
  60.6 0.0 reduce-scatter.24.cloned.1.call-start
  60.7 55.4 %all-reduce.4.cloned.1.call-done = f32[2048,32]{0,1:T(8,128)} async-done(((f32[2048,32]{0,1:T(8,128)}), f32[2048,32]{0,1:T(8,128)}) %all-reduce.4.cloned.1.call-update) | async-done | bytes 262160 | tf_op jit(solution)/shard_map/psum | solution.py:54
  116.1 5.2 %multiply_reduce_fusion.4 = (f32[32]{0:T(128)S(1)}, f32[32,2048]{1,0:T(8,128)S(1)}) fusion(f32[32]{0:T(128)S(1)} %broadcast_multiply_fusion, bf16[2048,2048]{1,0:T(8,128)(2,1)} %param.6, f32[2048,32]{0,1:T(8,128)} %all-reduce.4.cloned.1.call-done, f32[32]{0:T(128)S(1)} %get-tuple-element.32), kind=kOutput, calls=%fused_computation.31 | convolution fusion | flops 268763104 | bytes 8913280 | tf_op jit(solution)/shard_map/dot_general | solution.py:23
  121.3 6.0 %fusion = bf16[2048,32]{0,1:T(8,128)(2,1)S(1)} fusion(bf16[2048,2048]{1,0:T(8,128)(2,1)} %param.6, f32[32,2048]{1,0:T(8,128)S(1)} %get-tuple-element.34, f32[32]{0:T(128)S(1)} %get-tuple-element.30), kind=kOutput, calls=%fused_computation.10 | convolution fusion | flops 268632064 | bytes 8781952 | tf_op jit(solution)/shard_map/dot_general | solution.py:57
  127.3 14.9 %all_gather.18 = bf16[2048,128]{0,1:T(8,128)(2,1)S(1)} all-gather(bf16[2048,32]{0,1:T(8,128)(2,1)S(1)} %fusion), channel_id=1, replica_groups=mesh['rows'=8,'grp'=4] {'grp'}, dimensions={1}, use_global_device_ids=true | all-gather | bytes 655360 | tf_op jit(solution)/shard_map/all_gather | solution.py:60
  142.2 11.7 %all-gather = f32[4,32,2]{1,2,0:T(2,128)S(1)} all-gather(f32[1,32,2]{1,2,0:T(2,128)S(1)} %maximum_bitcast_fusion), channel_id=1, replica_groups=mesh['rows'=8,'grp'=4] {'grp'}, dimensions={0}, use_global_device_ids=true | all-gather | bytes 1280 | tf_op jit(solution)/shard_map/all_gather | solution.py:61
  153.9 0.1 reshape.67
  154.0 0.9 multiply_reduce_fusion.3
  154.9 0.8 copy.18
  155.7 0.0 reduce-scatter.24.cloned.1.call-update
  155.7 0.0 reduce-scatter.18.cloned.1.call-start
  155.8 1.4 convolution_bitcast_fusion.1
  157.2 0.0 reduce-scatter.18.cloned.1.call-update
  157.2 0.0 all-reduce.6.cloned.1.call-start
  157.3 14.5 %reduce-scatter.24.cloned.1.call-done = f32[32,1]{1,0:T(8,128)} async-done(((f32[128,1]{1,0:T(8,128)}), f32[32,1]{1,0:T(8,128)}) %reduce-scatter.24.cloned.1.call-update) | async-done | bytes 144
  171.8 0.8 copy.19
  172.5 11.9 %psum.51 = f32[1,32]{1,0:T(1,128)S(1)} all-reduce(f32[1,32]{1,0:T(1,128)S(1)} %copy.19), channel_id=1, replica_groups=mesh['rows'=8,'grp'=4] {'rows'}, use_global_device_ids=true, to_apply=%region_8.0 | all-reduce | flops 32 | bytes 256 | tf_op jit(solution)/shard_map/psum | solution.py:54
  184.4 15.0 %reduce-scatter.18.cloned.1.call-done = f32[2048,32]{0,1:T(8,128)} async-done(((f32[2048,128]{0,1:T(8,128)}), f32[2048,32]{0,1:T(8,128)}) %reduce-scatter.18.cloned.1.call-update) | async-done | bytes 262160 | tf_op jit(solution)/shard_map/reduce_scatter | solution.py:51
  199.4 0.0 all-reduce.6.cloned.1.call-update
  199.4 0.0 reduce-scatter.26.cloned.1.call-start
  199.5 55.2 %all-reduce.6.cloned.1.call-done = f32[2048,32]{0,1:T(8,128)} async-done(((f32[2048,32]{0,1:T(8,128)}), f32[2048,32]{0,1:T(8,128)}) %all-reduce.6.cloned.1.call-update) | async-done | bytes 262160 | tf_op jit(solution)/shard_map/psum | solution.py:54
  254.7 5.2 %multiply_reduce_fusion.1 = (f32[32]{0:T(128)S(1)}, f32[32,2048]{1,0:T(8,128)S(1)}) fusion(f32[32,2048]{1,0:T(8,128)S(1)} %get-tuple-element.34, f32[32]{0:T(128)S(1)} %get-tuple-element.30, f32[32]{0:T(128)S(1)} %get-tuple-element.28, bf16[2048,2048]{1,0:T(8,128)(2,1)} %param.6, f32[2048,32]{0,1:T(8,128)} %all-reduce.6.cloned.1.call-done), kind=kOutput, calls=%fused_computation.26 | convolution fusion | flops 268894176 | bytes 9175424 | tf_op jit(solution)/shard_map/dot_general | solution.py:23
  259.9 6.0 %fusion.1 = bf16[2048,32]{0,1:T(8,128)(2,1)S(1)} fusion(bf16[2048,2048]{1,0:T(8,128)(2,1)} %param.6, f32[32,2048]{1,0:T(8,128)S(1)} %get-tuple-element.38, f32[32]{0:T(128)S(1)} %get-tuple-element.26), kind=kOutput, calls=%fused_computation.11 | convolution fusion | flops 268632064 | bytes 8781952 | tf_op jit(solution)/shard_map/dot_general | solution.py:57
  265.9 14.9 %all_gather.20 = bf16[2048,128]{0,1:T(8,128)(2,1)S(1)} all-gather(bf16[2048,32]{0,1:T(8,128)(2,1)S(1)} %fusion.1), channel_id=1, replica_groups=mesh['rows'=8,'grp'=4] {'grp'}, dimensions={1}, use_global_device_ids=true | all-gather | bytes 655360 | tf_op jit(solution)/shard_map/all_gather | solution.py:60
  280.9 11.7 %all-gather.1 = f32[4,32,2]{1,2,0:T(2,128)S(1)} all-gather(f32[1,32,2]{1,2,0:T(2,128)S(1)} %maximum_bitcast_fusion.1), channel_id=1, replica_groups=mesh['rows'=8,'grp'=4] {'grp'}, dimensions={0}, use_global_device_ids=true | all-gather | bytes 1280 | tf_op jit(solution)/shard_map/all_gather | solution.py:61
  292.5 0.1 reshape.69
  292.6 1.5 multiply_reduce_fusion.2
  294.2 0.7 copy.20
  294.9 0.0 reduce-scatter.26.cloned.1.call-update
  295.0 0.0 reduce-scatter.20.cloned.1.call-start
  295.0 2.4 convolution_bitcast_fusion
  297.4 0.0 reduce-scatter.20.cloned.1.call-update
  297.4 0.0 all-reduce.8.cloned.1.call-start
  297.5 13.5 %reduce-scatter.26.cloned.1.call-done = f32[32,1]{1,0:T(8,128)} async-done(((f32[128,1]{1,0:T(8,128)}), f32[32,1]{1,0:T(8,128)}) %reduce-scatter.26.cloned.1.call-update) | async-done | bytes 144
  311.0 0.8 copy.21
  311.8 11.8 %psum.53 = f32[1,32]{1,0:T(1,128)S(1)} all-reduce(f32[1,32]{1,0:T(1,128)S(1)} %copy.21), channel_id=1, replica_groups=mesh['rows'=8,'grp'=4] {'rows'}, use_global_device_ids=true, to_apply=%region_14.0 | all-reduce | flops 32 | bytes 256 | tf_op jit(solution)/shard_map/psum | solution.py:54
  323.6 15.2 %reduce-scatter.20.cloned.1.call-done = f32[2048,32]{0,1:T(8,128)} async-done(((f32[2048,128]{0,1:T(8,128)}), f32[2048,32]{0,1:T(8,128)}) %reduce-scatter.20.cloned.1.call-update) | async-done | bytes 262160 | tf_op jit(solution)/shard_map/reduce_scatter | solution.py:51
  338.8 0.0 reduce-scatter.28.cloned.1.call-start
  338.8 55.4 %all-reduce.8.cloned.1.call-done = f32[2048,32]{0,1:T(8,128)} async-done(((f32[2048,32]{0,1:T(8,128)}), f32[2048,32]{0,1:T(8,128)}) %all-reduce.8.cloned.1.call-update) | async-done | bytes 262160 | tf_op jit(solution)/shard_map/psum | solution.py:54
  394.2 5.2 %multiply_reduce_fusion = (f32[32]{0:T(128)S(1)}, f32[32,2048]{1,0:T(8,128)S(1)}) fusion(f32[32,2048]{1,0:T(8,128)S(1)} %get-tuple-element.38, f32[32]{0:T(128)S(1)} %get-tuple-element.26, f32[32]{0:T(128)S(1)} %get-tuple-element.24, bf16[2048,2048]{1,0:T(8,128)(2,1)} %param.6, f32[2048,32]{0,1:T(8,128)} %all-reduce.8.cloned.1.call-done), kind=kOutput, calls=%fused_computation.25 | convolution fusion | flops 268894176 | bytes 9175424 | tf_op jit(solution)/shard_map/dot_general | solution.py:23
  399.4 11.2 %all-gather.2 = f32[4,32,2]{1,2,0:T(2,128)S(1)} all-gather(f32[1,32,2]{1,2,0:T(2,128)S(1)} %maximum_bitcast_fusion.2), channel_id=1, replica_groups=mesh['rows'=8,'grp'=4] {'grp'}, dimensions={0}, use_global_device_ids=true | all-gather | bytes 1280 | tf_op jit(solution)/shard_map/all_gather | solution.py:61
  410.7 0.1 reshape.71
  410.8 6.0 %fusion.2 = bf16[2048,32]{0,1:T(8,128)(2,1)S(1)} fusion(bf16[2048,2048]{1,0:T(8,128)(2,1)} %param.6, f32[32,2048]{1,0:T(8,128)S(1)} %get-tuple-element.42, f32[32]{0:T(128)S(1)} %get-tuple-element.22), kind=kOutput, calls=%fused_computation.12 | convolution fusion | flops 268632064 | bytes 8781952 | tf_op jit(solution)/shard_map/dot_general | solution.py:57
  416.8 14.8 %all_gather.22 = bf16[2048,128]{0,1:T(8,128)(2,1)S(1)} all-gather(bf16[2048,32]{0,1:T(8,128)(2,1)S(1)} %fusion.2), channel_id=1, replica_groups=mesh['rows'=8,'grp'=4] {'grp'}, dimensions={1}, use_global_device_ids=true | all-gather | bytes 655360 | tf_op jit(solution)/shard_map/all_gather | solution.py:60
  431.5 0.9 fusion.10
  432.5 0.8 copy.22
  433.2 16.8 %reduce-scatter.28.cloned.1.call-done = f32[32,1]{1,0:T(8,128)} async-done(((f32[128,1]{1,0:T(8,128)}), f32[32,1]{1,0:T(8,128)}) %reduce-scatter.28.cloned.1.call-update) | async-done | bytes 144
  450.0 0.8 copy.23
  450.8 11.8 %psum.55 = f32[1,32]{1,0:T(1,128)S(1)} all-reduce(f32[1,32]{1,0:T(1,128)S(1)} %copy.23), channel_id=1, replica_groups=mesh['rows'=8,'grp'=4] {'rows'}, use_global_device_ids=true, to_apply=%region_20.0 | all-reduce | flops 32 | bytes 256 | tf_op jit(solution)/shard_map/psum | solution.py:54
  462.6 0.6 fusion.29
  463.2 0.2 add_bitcast_fusion
  463.4 6.8 %convolution_bitcast_fusion.3 = f32[2048,32]{0,1:T(8,128)} fusion(bf16[2048,2048]{1,0:T(8,128)(2,1)} %param.6, f32[2048,32]{0,1:T(8,128)S(1)} %add_bitcast_fusion), kind=kOutput, calls=%fused_computation.3 | convolution fusion | flops 268500992 | bytes 8912896 | tf_op jit(solution)/shard_map/dot_general | solution.py:95
  (28 shorter events, 0.2 us)
Async XLA Ops:
  7.2 2.8 copy-start
  7.2 25.6 %reduce-scatter.22.cloned.1.call-start = ((), (), s32[]{:S(2)}) async-start(), calls=%async_computation.13 | async-start | bytes 81920
  9.9 50.7 %reduce-scatter.16.cloned.1.call-start = ((), (), s32[]{:S(2)}) async-start(), calls=%async_computation.7 | async-start | bytes 1310720 | tf_op jit(solution)/shard_map/reduce_scatter | solution.py:51
  11.5 104.6 %all-reduce.4.cloned.1.call-start = ((), (), s32[]{:S(2)}) async-start(), calls=%async_computation.8 | async-start | bytes 524288 | tf_op jit(solution)/shard_map/psum | solution.py:54
  60.6 111.1 %reduce-scatter.24.cloned.1.call-start = ((), (), s32[]{:S(2)}) async-start(), calls=%async_computation.14 | async-start | bytes 81920
  155.7 43.7 %reduce-scatter.18.cloned.1.call-start = ((), (), s32[]{:S(2)}) async-start(), calls=%async_computation.9 | async-start | bytes 1310720 | tf_op jit(solution)/shard_map/reduce_scatter | solution.py:51
  157.2 97.5 %all-reduce.6.cloned.1.call-start = ((), (), s32[]{:S(2)}) async-start(), calls=%async_computation.10 | async-start | bytes 524288 | tf_op jit(solution)/shard_map/psum | solution.py:54
  199.4 111.5 %reduce-scatter.26.cloned.1.call-start = ((), (), s32[]{:S(2)}) async-start(), calls=%async_computation.15 | async-start | bytes 81920
  295.0 43.8 %reduce-scatter.20.cloned.1.call-start = ((), (), s32[]{:S(2)}) async-start(), calls=%async_computation.11 | async-start | bytes 1310720 | tf_op jit(solution)/shard_map/reduce_scatter | solution.py:51
  297.4 96.8 %all-reduce.8.cloned.1.call-start = ((), (), s32[]{:S(2)}) async-start(), calls=%async_computation.12 | async-start | bytes 524288 | tf_op jit(solution)/shard_map/psum | solution.py:54
  338.8 111.2 %reduce-scatter.28.cloned.1.call-start = ((), (), s32[]{:S(2)}) async-start(), calls=%async_computation.16 | async-start | bytes 81920
  399.4 32.1 %copy-start.2 = (f32[512,128]{0,1:T(8,128)S(1)}, f32[512,128]{0,1:T(8,128)}, u32[]{:S(2)}) copy-start(f32[512,128]{0,1:T(8,128)} %get-tuple-element.40) | copy-start | bytes 786436
  463.4 6.8 %copy-start.1 = (f32[2048,32]{0,1:T(8,128)}, f32[2048,32]{0,1:T(8,128)S(1)}, u32[]{:S(2)}) copy-start(f32[2048,32]{0,1:T(8,128)S(1)} %add_bitcast_fusion) | copy-start | bytes 786436
Sparse Core Ops, SparseCore 0:
  10.8 21.9 reduce-scatter.21
  35.1 25.4 reduce-scatter.15
  63.7 52.3 all-reduce.3
  155.8 15.8 reduce-scatter.23
  173.9 25.4 reduce-scatter.17
  202.3 52.3 all-reduce.5
  295.1 15.8 reduce-scatter.25
  313.3 25.4 reduce-scatter.19
  341.8 52.3 all-reduce.7
  433.4 16.6 reduce-scatter.27
where the time goes:
time: 478 us; the launch traced here: 477 us
  waiting for transfers between devices  278 us (58%)
  blocking collectives  127 us (27%)
  matrix products  49 us (10%)
  between operations  15.1 us (3%)
  local copies, waits for them, and re-layouts  7.48 us (2%)
    psum x3, waiting for transfers between devices, reduce_cols(): return lax.psum((shared, shared_sq), 'rows')  166 us
    unnamed x14, waiting for transfers between devices  66.2 us
    psum x4, blocking collectives, reduce_cols(): return lax.psum((shared, shared_sq), 'rows')  47.4 us
    reduce_scatter x3, waiting for transfers between devices, reduce_cols(): lax.psum_scatter(partial_value, 'grp', scatter_dimension=1, tiled=True)  45.3 us
    all_gather x3, blocking collectives, share_cols(): pushed = lax.all_gather(pushed, 'grp', axis=1, tiled=True)  44.6 us
    all_gather x3, blocking collectives, share_cols(): lax.all_gather(jnp.concatenate([v_norm, u_norm], axis=0), 'grp', axis=1,...  34.6 us
    dot_general x3, matrix products, share_cols(): jnp.dot(precond, right_vec.astype(jnp.bfloat16), preferred_element_type=j...  18 us
    dot_general x3, matrix products, column_section(): lax.dot_general(precond, (partial_value / u_norm).astype(jnp.bfloat16), (...  15.6 us
  transfers between devices with their start and end apart: 10, of which 10 were waited for; matrix products, arithmetic and copies ran while one was open for 2% of the time, Pallas kernels for 0%

commit v1 on v0

--- a/solution.py
+++ b/solution.py
@@ -57,7 +57,14 @@
         pushed = jnp.dot(
             precond, right_vec.astype(jnp.bfloat16), preferred_element_type=jnp.float32
         ).astype(jnp.bfloat16)
-        pushed = lax.all_gather(pushed, "grp", axis=1, tiled=True)
+        ring = [pushed]
+        for hop in range(3):
+            ring.append(lax.ppermute(ring[-1], "grp", [(dev, (dev + 1) % 4) for dev in range(4)]))
+        pushed = jnp.roll(
+            jnp.concatenate(ring[::-1], axis=1),
+            (lax.axis_index("grp") + 1) * ring[0].shape[1],
+            axis=1,
+        )
         norms = lax.all_gather(jnp.concatenate([v_norm, u_norm], axis=0), "grp", axis=1, tiled=True)
         return (pushed, norms[0:1], norms[1:2])
 

time: 478 us -> 476 us (level)
  blocking collectives: 127 us -> 81.5 us
  waiting for transfers between devices: 278 us -> 314 us
    all_gather x3 -> x0, blocking collectives: 44.6 us -> none  [share_cols(): pushed = lax.all_gather(pushed, 'grp', axis=1, tiled=True)]
    ppermute x0 -> x9, waiting for transfers between devices: none -> 36.5 us  [share_cols(): lax.ppermute(ring[-1], 'grp', [(dev, (dev + 1) % 4) for dev in range(4)])]
  transfers between devices with their start and end apart: 10 -> 19, of which waited for: 10 -> 16; matrix products, arithmetic and copies ran while one was open for 2% -> 1% of each run, Pallas kernels for 0% -> 0%
where the time goes in v1:
time: 476 us
  waiting for transfers between devices  314 us (66%)
  blocking collectives  81.5 us (17%)
  matrix products  50.9 us (11%)
  between operations  15.1 us (3%)
  local copies, waits for them, and re-layouts  7.47 us (2%)
  starting transfers between devices  5.17 us (1%)
    psum x3, waiting for transfers between devices, reduce_cols(): return lax.psum((shared, shared_sq), 'rows')  166 us
    unnamed x14, waiting for transfers between devices  66.6 us
    psum x4, blocking collectives, reduce_cols(): return lax.psum((shared, shared_sq), 'rows')  47.4 us
    reduce_scatter x3, waiting for transfers between devices, reduce_cols(): lax.psum_scatter(partial_value, 'grp', scatter_dimension=1, tiled=True)  45.2 us
    ppermute x9, waiting for transfers between devices, share_cols(): lax.ppermute(ring[-1], 'grp', [(dev, (dev + 1) % 4) for dev in range(4)])  36.5 us
    all_gather x3, blocking collectives, share_cols(): lax.all_gather(jnp.concatenate([v_norm, u_norm], axis=0), 'grp', axis=1,...  34.1 us
    dot_general x3, matrix products, share_cols(): jnp.dot(precond, right_vec.astype(jnp.bfloat16), preferred_element_type=j...  18 us
    dot_general x3, matrix products, column_section(): lax.dot_general(precond, (partial_value / u_norm).astype(jnp.bfloat16), (...  15.6 us
  transfers between devices with their start and end apart: 19, of which 16 were waited for; matrix products, arithmetic and copies ran while one was open for 1% of the time, Pallas kernels for 0%

profile of v1, /device:TPU:0, one launch (start us, length us, event | category | flops | bytes accessed | tf_op | source)
XLA Modules:
  0.0 475.5 jit_solution(12150839187732953643)
XLA Ops:
  8.0 1.0 copy.12
  9.0 0.1 multiply_reduce_fusion.5
  9.2 0.7 copy.16
  9.9 0.0 reduce-scatter.16.cloned.1.call-start
  10.0 1.4 convolution_bitcast_fusion.2
  11.5 0.0 all-reduce.4.cloned.1.call-start
  11.5 21.3 %reduce-scatter.22.cloned.1.call-done = f32[32,1]{1,0:T(8,128)} async-done(((f32[128,1]{1,0:T(8,128)}), f32[32,1]{1,0:T(8,128)}) %reduce-scatter.22.cloned.1.call-update) | async-done | bytes 144
  32.8 0.8 copy.17
  33.6 11.8 %psum.50 = f32[1,32]{1,0:T(1,128)S(1)} all-reduce(f32[1,32]{1,0:T(1,128)S(1)} %copy.17), channel_id=1, replica_groups=mesh['rows'=8,'grp'=4] {'rows'}, use_global_device_ids=true, to_apply=%region_4.0 | all-reduce | flops 32 | bytes 256 | tf_op jit(solution)/shard_map/psum | solution.py:54
  45.5 15.1 %reduce-scatter.16.cloned.1.call-done = f32[2048,32]{0,1:T(8,128)} async-done(((f32[2048,128]{0,1:T(8,128)}), f32[2048,32]{0,1:T(8,128)}) %reduce-scatter.16.cloned.1.call-update) | async-done | bytes 262160 | tf_op jit(solution)/shard_map/reduce_scatter | solution.py:51
  60.6 0.0 reduce-scatter.24.cloned.1.call-start
  60.7 55.4 %all-reduce.4.cloned.1.call-done = f32[2048,32]{0,1:T(8,128)} async-done(((f32[2048,32]{0,1:T(8,128)}), f32[2048,32]{0,1:T(8,128)}) %all-reduce.4.cloned.1.call-update) | async-done | bytes 262160 | tf_op jit(solution)/shard_map/psum | solution.py:54
  116.1 5.2 %multiply_reduce_fusion.4 = (f32[32]{0:T(128)S(1)}, f32[32,2048]{1,0:T(8,128)S(1)}) fusion(f32[32]{0:T(128)S(1)} %broadcast_multiply_fusion, bf16[2048,2048]{1,0:T(8,128)(2,1)} %param.8, f32[2048,32]{0,1:T(8,128)} %all-reduce.4.cloned.1.call-done, f32[32]{0:T(128)S(1)} %get-tuple-element.33), kind=kOutput, calls=%fused_computation.76 | convolution fusion | flops 268763104 | bytes 8913280 | tf_op jit(solution)/shard_map/dot_general | solution.py:23
  121.3 6.0 %fusion = bf16[2048,32]{0,1:T(8,128)(2,1)S(1)} fusion(bf16[2048,2048]{1,0:T(8,128)(2,1)} %param.8, f32[32,2048]{1,0:T(8,128)S(1)} %get-tuple-element.35, f32[32]{0:T(128)S(1)} %get-tuple-element.31), kind=kOutput, calls=%fused_computation.10 | convolution fusion | flops 268632064 | bytes 8781952 | tf_op jit(solution)/shard_map/dot_general | solution.py:57
  127.3 1.5 collective-permute-start
  128.8 5.3 %collective-permute-done = bf16[2048,32]{0,1:T(8,128)(2,1)S(1)} collective-permute-done((bf16[2048,32]{0,1:T(8,128)(2,1)S(1)}, bf16[2048,32]{0,1:T(8,128)(2,1)S(1)}, u32[]{:S(2)}, u32[]{:S(2)}) %collective-permute-start) | collective-permute-done | bytes 131104 | tf_op jit(solution)/shard_map/ppermute | solution.py:62
  134.1 11.4 %all-gather = f32[4,32,2]{1,2,0:T(2,128)S(1)} all-gather(f32[1,32,2]{1,2,0:T(2,128)S(1)} %maximum_bitcast_fusion), channel_id=1, replica_groups=mesh['rows'=8,'grp'=4] {'grp'}, dimensions={0}, use_global_device_ids=true | all-gather | bytes 1280 | tf_op jit(solution)/shard_map/all_gather | solution.py:68
  145.5 0.1 reshape.67
  145.6 6.8 %collective-permute-done.2 = bf16[2048,32]{0,1:T(8,128)(2,1)S(1)} collective-permute-done((bf16[2048,32]{0,1:T(8,128)(2,1)S(1)}, bf16[2048,32]{0,1:T(8,128)(2,1)S(1)}, u32[]{:S(2)}, u32[]{:S(2)}) %collective-permute-start.2) | collective-permute-done | bytes 131104 | tf_op jit(solution)/shard_map/ppermute | solution.py:62
  152.4 1.6 multiply_reduce_fusion.3
  154.0 0.8 copy.18
  154.8 0.0 reduce-scatter.18.cloned.1.call-start
  154.8 1.4 convolution_bitcast_fusion.1
  156.3 0.0 all-reduce.6.cloned.1.call-start
  156.3 14.5 %reduce-scatter.24.cloned.1.call-done = f32[32,1]{1,0:T(8,128)} async-done(((f32[128,1]{1,0:T(8,128)}), f32[32,1]{1,0:T(8,128)}) %reduce-scatter.24.cloned.1.call-update) | async-done | bytes 144
  170.8 0.8 copy.19
  171.6 11.9 %psum.51 = f32[1,32]{1,0:T(1,128)S(1)} all-reduce(f32[1,32]{1,0:T(1,128)S(1)} %copy.19), channel_id=1, replica_groups=mesh['rows'=8,'grp'=4] {'rows'}, use_global_device_ids=true, to_apply=%region_8.10 | all-reduce | flops 32 | bytes 256 | tf_op jit(solution)/shard_map/psum | solution.py:54
  183.5 15.0 %reduce-scatter.18.cloned.1.call-done = f32[2048,32]{0,1:T(8,128)} async-done(((f32[2048,128]{0,1:T(8,128)}), f32[2048,32]{0,1:T(8,128)}) %reduce-scatter.18.cloned.1.call-update) | async-done | bytes 262160 | tf_op jit(solution)/shard_map/reduce_scatter | solution.py:51
  198.5 0.0 reduce-scatter.26.cloned.1.call-start
  198.5 55.2 %all-reduce.6.cloned.1.call-done = f32[2048,32]{0,1:T(8,128)} async-done(((f32[2048,32]{0,1:T(8,128)}), f32[2048,32]{0,1:T(8,128)}) %all-reduce.6.cloned.1.call-update) | async-done | bytes 262160 | tf_op jit(solution)/shard_map/psum | solution.py:54
  253.8 5.2 %multiply_reduce_fusion.1 = (f32[32]{0:T(128)S(1)}, f32[32,2048]{1,0:T(8,128)S(1)}) fusion(f32[32,2048]{1,0:T(8,128)S(1)} %get-tuple-element.35, f32[32]{0:T(128)S(1)} %get-tuple-element.31, f32[32]{0:T(128)S(1)} %get-tuple-element.29, bf16[2048,2048]{1,0:T(8,128)(2,1)} %param.8, f32[2048,32]{0,1:T(8,128)} %all-reduce.6.cloned.1.call-done), kind=kOutput, calls=%fused_computation.71 | convolution fusion | flops 268894176 | bytes 9175424 | tf_op jit(solution)/shard_map/dot_general | solution.py:23
  259.0 6.0 %fusion.1 = bf16[2048,32]{0,1:T(8,128)(2,1)S(1)} fusion(bf16[2048,2048]{1,0:T(8,128)(2,1)} %param.8, f32[32,2048]{1,0:T(8,128)S(1)} %get-tuple-element.39, f32[32]{0:T(128)S(1)} %get-tuple-element.27), kind=kOutput, calls=%fused_computation.11 | convolution fusion | flops 268632064 | bytes 8781952 | tf_op jit(solution)/shard_map/dot_general | solution.py:57
  265.0 1.5 collective-permute-start.3
  266.5 5.3 %collective-permute-done.3 = bf16[2048,32]{0,1:T(8,128)(2,1)S(1)} collective-permute-done((bf16[2048,32]{0,1:T(8,128)(2,1)S(1)}, bf16[2048,32]{0,1:T(8,128)(2,1)S(1)}, u32[]{:S(2)}, u32[]{:S(2)}) %collective-permute-start.3) | collective-permute-done | bytes 131104 | tf_op jit(solution)/shard_map/ppermute | solution.py:62
  271.8 11.4 %all-gather.1 = f32[4,32,2]{1,2,0:T(2,128)S(1)} all-gather(f32[1,32,2]{1,2,0:T(2,128)S(1)} %maximum_bitcast_fusion.1), channel_id=1, replica_groups=mesh['rows'=8,'grp'=4] {'grp'}, dimensions={0}, use_global_device_ids=true | all-gather | bytes 1280 | tf_op jit(solution)/shard_map/all_gather | solution.py:68
  283.2 0.1 reshape.69
  283.3 0.2 collective-permute-start.5
  283.5 7.0 %collective-permute-done.5 = bf16[2048,32]{0,1:T(8,128)(2,1)S(1)} collective-permute-done((bf16[2048,32]{0,1:T(8,128)(2,1)}, bf16[2048,32]{0,1:T(8,128)(2,1)S(1)}, u32[]{:S(2)}, u32[]{:S(2)}) %collective-permute-start.5) | collective-permute-done | bytes 131104 | tf_op jit(solution)/shard_map/ppermute | solution.py:62
  290.5 2.3 multiply_reduce_fusion.2
  292.8 0.8 copy.20
  293.6 0.0 reduce-scatter.20.cloned.1.call-start
  293.6 1.4 convolution_bitcast_fusion
  295.1 0.0 all-reduce.8.cloned.1.call-start
  295.1 14.5 %reduce-scatter.26.cloned.1.call-done = f32[32,1]{1,0:T(8,128)} async-done(((f32[128,1]{1,0:T(8,128)}), f32[32,1]{1,0:T(8,128)}) %reduce-scatter.26.cloned.1.call-update) | async-done | bytes 144
  309.6 0.8 copy.21
  310.4 11.8 %psum.53 = f32[1,32]{1,0:T(1,128)S(1)} all-reduce(f32[1,32]{1,0:T(1,128)S(1)} %copy.21), channel_id=1, replica_groups=mesh['rows'=8,'grp'=4] {'rows'}, use_global_device_ids=true, to_apply=%region_14.16 | all-reduce | flops 32 | bytes 256 | tf_op jit(solution)/shard_map/psum | solution.py:54
  322.3 15.1 %reduce-scatter.20.cloned.1.call-done = f32[2048,32]{0,1:T(8,128)} async-done(((f32[2048,128]{0,1:T(8,128)}), f32[2048,32]{0,1:T(8,128)}) %reduce-scatter.20.cloned.1.call-update) | async-done | bytes 262160 | tf_op jit(solution)/shard_map/reduce_scatter | solution.py:51
  337.4 0.0 reduce-scatter.28.cloned.1.call-start
  337.5 55.4 %all-reduce.8.cloned.1.call-done = f32[2048,32]{0,1:T(8,128)} async-done(((f32[2048,32]{0,1:T(8,128)}), f32[2048,32]{0,1:T(8,128)}) %all-reduce.8.cloned.1.call-update) | async-done | bytes 262160 | tf_op jit(solution)/shard_map/psum | solution.py:54
  392.8 5.2 %multiply_reduce_fusion = (f32[32]{0:T(128)S(1)}, f32[32,2048]{1,0:T(8,128)S(1)}) fusion(f32[32,2048]{1,0:T(8,128)S(1)} %get-tuple-element.39, f32[32]{0:T(128)S(1)} %get-tuple-element.27, f32[32]{0:T(128)S(1)} %get-tuple-element.25, bf16[2048,2048]{1,0:T(8,128)(2,1)} %param.8, f32[2048,32]{0,1:T(8,128)} %all-reduce.8.cloned.1.call-done), kind=kOutput, calls=%fused_computation.70 | convolution fusion | flops 268894176 | bytes 9175424 | tf_op jit(solution)/shard_map/dot_general | solution.py:23
  398.1 6.0 %fusion.2 = bf16[2048,32]{0,1:T(8,128)(2,1)S(1)} fusion(bf16[2048,2048]{1,0:T(8,128)(2,1)} %param.8, f32[32,2048]{1,0:T(8,128)S(1)} %get-tuple-element.43, f32[32]{0:T(128)S(1)} %get-tuple-element.23), kind=kOutput, calls=%fused_computation.12 | convolution fusion | flops 268632064 | bytes 8781952 | tf_op jit(solution)/shard_map/dot_general | solution.py:57
  404.1 1.5 collective-permute-start.6
  405.6 5.3 %collective-permute-done.6 = bf16[2048,32]{0,1:T(8,128)(2,1)S(1)} collective-permute-done((bf16[2048,32]{0,1:T(8,128)(2,1)S(1)}, bf16[2048,32]{0,1:T(8,128)(2,1)S(1)}, u32[]{:S(2)}, u32[]{:S(2)}) %collective-permute-start.6) | collective-permute-done | bytes 131104 | tf_op jit(solution)/shard_map/ppermute | solution.py:62
  410.9 11.4 %all-gather.2 = f32[4,32,2]{1,2,0:T(2,128)S(1)} all-gather(f32[1,32,2]{1,2,0:T(2,128)S(1)} %maximum_bitcast_fusion.2), channel_id=1, replica_groups=mesh['rows'=8,'grp'=4] {'grp'}, dimensions={0}, use_global_device_ids=true | all-gather | bytes 1280 | tf_op jit(solution)/shard_map/all_gather | solution.py:68
  422.3 0.1 reshape.71
  422.4 7.0 %collective-permute-done.8 = bf16[2048,32]{0,1:T(8,128)(2,1)S(1)} collective-permute-done((bf16[2048,32]{0,1:T(8,128)(2,1)}, bf16[2048,32]{0,1:T(8,128)(2,1)S(1)}, u32[]{:S(2)}, u32[]{:S(2)}) %collective-permute-start.8) | collective-permute-done | bytes 131104 | tf_op jit(solution)/shard_map/ppermute | solution.py:62
  429.3 2.3 fusion.10
  431.6 0.8 copy.22
  432.4 16.1 %reduce-scatter.28.cloned.1.call-done = f32[32,1]{1,0:T(8,128)} async-done(((f32[128,1]{1,0:T(8,128)}), f32[32,1]{1,0:T(8,128)}) %reduce-scatter.28.cloned.1.call-update) | async-done | bytes 144
  448.5 0.8 copy.23
  449.3 11.8 %psum.55 = f32[1,32]{1,0:T(1,128)S(1)} all-reduce(f32[1,32]{1,0:T(1,128)S(1)} %copy.23), channel_id=1, replica_groups=mesh['rows'=8,'grp'=4] {'rows'}, use_global_device_ids=true, to_apply=%region_20.22 | all-reduce | flops 32 | bytes 256 | tf_op jit(solution)/shard_map/psum | solution.py:54
  461.1 0.6 fusion.59
  461.7 0.2 add_bitcast_fusion
  461.9 6.8 %convolution_bitcast_fusion.3 = f32[2048,32]{0,1:T(8,128)} fusion(bf16[2048,2048]{1,0:T(8,128)(2,1)} %param.8, f32[2048,32]{0,1:T(8,128)S(1)} %add_bitcast_fusion), kind=kOutput, calls=%fused_computation.3 | convolution fusion | flops 268500992 | bytes 8912896 | tf_op jit(solution)/shard_map/dot_general | solution.py:102
  (41 shorter events, 0.4 us)
Async XLA Ops:
  7.2 2.8 copy-start
  7.2 25.6 %reduce-scatter.22.cloned.1.call-start = ((), (), s32[]{:S(2)}) async-start(), calls=%async_computation.13 | async-start | bytes 81920
  9.9 50.7 %reduce-scatter.16.cloned.1.call-start = ((), (), s32[]{:S(2)}) async-start(), calls=%async_computation.7 | async-start | bytes 1310720 | tf_op jit(solution)/shard_map/reduce_scatter | solution.py:51
  11.5 104.6 %all-reduce.4.cloned.1.call-start = ((), (), s32[]{:S(2)}) async-start(), calls=%async_computation.8 | async-start | bytes 524288 | tf_op jit(solution)/shard_map/psum | solution.py:54
  60.6 110.2 %reduce-scatter.24.cloned.1.call-start = ((), (), s32[]{:S(2)}) async-start(), calls=%async_computation.14 | async-start | bytes 81920
  127.3 6.8 %collective-permute-start = (bf16[2048,32]{0,1:T(8,128)(2,1)S(1)}, bf16[2048,32]{0,1:T(8,128)(2,1)S(1)}, u32[]{:S(2)}, u32[]{:S(2)}) collective-permute-start(bf16[2048,32]{0,1:T(8,128)(2,1)S(1)} %fusion), channel_id=1, source_target_pairs={{0,1},{1,2},{2,3},{3,0},{4,5},{5,6},{6,7},{7,4},{8,9},{9,10},{10,1... | collective-permute-start | bytes 393224 | tf_op jit(solution)/shard_map/ppermute | solution.py:62
  134.1 11.5 %collective-permute-start.1 = (bf16[2048,32]{0,1:T(8,128)(2,1)S(1)}, bf16[2048,32]{0,1:T(8,128)(2,1)S(1)}, u32[]{:S(2)}, u32[]{:S(2)}) collective-permute-start(bf16[2048,32]{0,1:T(8,128)(2,1)S(1)} %collective-permute-done), channel_id=1, source_target_pairs={{0,1},{1,2},{2,3},{3,0},{4,5},{5,6},{6,7},{7,4},{8,9},{9,10},{10,1... | collective-permute-start | bytes 393224 | tf_op jit(solution)/shard_map/ppermute | solution.py:62
  145.6 6.8 %collective-permute-start.2 = (bf16[2048,32]{0,1:T(8,128)(2,1)S(1)}, bf16[2048,32]{0,1:T(8,128)(2,1)S(1)}, u32[]{:S(2)}, u32[]{:S(2)}) collective-permute-start(bf16[2048,32]{0,1:T(8,128)(2,1)S(1)} %collective-permute-done.1), channel_id=1, source_target_pairs={{0,1},{1,2},{2,3},{3,0},{4,5},{5,6},{6,7},{7,4},{8,9},{9,10},{10,1... | collective-permute-start | bytes 393224 | tf_op jit(solution)/shard_map/ppermute | solution.py:62
  154.8 43.7 %reduce-scatter.18.cloned.1.call-start = ((), (), s32[]{:S(2)}) async-start(), calls=%async_computation.9 | async-start | bytes 1310720 | tf_op jit(solution)/shard_map/reduce_scatter | solution.py:51
  156.3 97.5 %all-reduce.6.cloned.1.call-start = ((), (), s32[]{:S(2)}) async-start(), calls=%async_computation.10 | async-start | bytes 524288 | tf_op jit(solution)/shard_map/psum | solution.py:54
  198.5 111.2 %reduce-scatter.26.cloned.1.call-start = ((), (), s32[]{:S(2)}) async-start(), calls=%async_computation.15 | async-start | bytes 81920
  265.0 6.8 %collective-permute-start.3 = (bf16[2048,32]{0,1:T(8,128)(2,1)S(1)}, bf16[2048,32]{0,1:T(8,128)(2,1)S(1)}, u32[]{:S(2)}, u32[]{:S(2)}) collective-permute-start(bf16[2048,32]{0,1:T(8,128)(2,1)S(1)} %fusion.1), channel_id=1, source_target_pairs={{0,1},{1,2},{2,3},{3,0},{4,5},{5,6},{6,7},{7,4},{8,9},{9,10},{10,1... | collective-permute-start | bytes 393224 | tf_op jit(solution)/shard_map/ppermute | solution.py:62
  271.8 11.5 %collective-permute-start.4 = (bf16[2048,32]{0,1:T(8,128)(2,1)S(1)}, bf16[2048,32]{0,1:T(8,128)(2,1)}, u32[]{:S(2)}, u32[]{:S(2)}) collective-permute-start(bf16[2048,32]{0,1:T(8,128)(2,1)S(1)} %collective-permute-done.3), channel_id=1, source_target_pairs={{0,1},{1,2},{2,3},{3,0},{4,5},{5,6},{6,7},{7,4},{8,9},{9,10},{10,1... | collective-permute-start | bytes 393224 | tf_op jit(solution)/shard_map/ppermute | solution.py:62
  283.3 7.1 %collective-permute-start.5 = (bf16[2048,32]{0,1:T(8,128)(2,1)}, bf16[2048,32]{0,1:T(8,128)(2,1)S(1)}, u32[]{:S(2)}, u32[]{:S(2)}) collective-permute-start(bf16[2048,32]{0,1:T(8,128)(2,1)} %collective-permute-done.4), channel_id=1, source_target_pairs={{0,1},{1,2},{2,3},{3,0},{4,5},{5,6},{6,7},{7,4},{8,9},{9,10},{10,1... | collective-permute-start | bytes 393224 | tf_op jit(solution)/shard_map/ppermute | solution.py:62
  293.6 43.8 %reduce-scatter.20.cloned.1.call-start = ((), (), s32[]{:S(2)}) async-start(), calls=%async_computation.11 | async-start | bytes 1310720 | tf_op jit(solution)/shard_map/reduce_scatter | solution.py:51
  295.1 97.8 %all-reduce.8.cloned.1.call-start = ((), (), s32[]{:S(2)}) async-start(), calls=%async_computation.12 | async-start | bytes 524288 | tf_op jit(solution)/shard_map/psum | solution.py:54
  337.4 111.1 %reduce-scatter.28.cloned.1.call-start = ((), (), s32[]{:S(2)}) async-start(), calls=%async_computation.16 | async-start | bytes 81920
  404.1 6.8 %collective-permute-start.6 = (bf16[2048,32]{0,1:T(8,128)(2,1)S(1)}, bf16[2048,32]{0,1:T(8,128)(2,1)S(1)}, u32[]{:S(2)}, u32[]{:S(2)}) collective-permute-start(bf16[2048,32]{0,1:T(8,128)(2,1)S(1)} %fusion.2), channel_id=1, source_target_pairs={{0,1},{1,2},{2,3},{3,0},{4,5},{5,6},{6,7},{7,4},{8,9},{9,10},{10,1... | collective-permute-start | bytes 393224 | tf_op jit(solution)/shard_map/ppermute | solution.py:62
  410.9 11.5 %collective-permute-start.7 = (bf16[2048,32]{0,1:T(8,128)(2,1)S(1)}, bf16[2048,32]{0,1:T(8,128)(2,1)}, u32[]{:S(2)}, u32[]{:S(2)}) collective-permute-start(bf16[2048,32]{0,1:T(8,128)(2,1)S(1)} %collective-permute-done.6), channel_id=1, source_target_pairs={{0,1},{1,2},{2,3},{3,0},{4,5},{5,6},{6,7},{7,4},{8,9},{9,10},{10,1... | collective-permute-start | bytes 393224 | tf_op jit(solution)/shard_map/ppermute | solution.py:62
  422.4 7.0 %collective-permute-start.8 = (bf16[2048,32]{0,1:T(8,128)(2,1)}, bf16[2048,32]{0,1:T(8,128)(2,1)S(1)}, u32[]{:S(2)}, u32[]{:S(2)}) collective-permute-start(bf16[2048,32]{0,1:T(8,128)(2,1)} %collective-permute-done.7), channel_id=1, source_target_pairs={{0,1},{1,2},{2,3},{3,0},{4,5},{5,6},{6,7},{7,4},{8,9},{9,10},{10,1... | collective-permute-start | bytes 393224 | tf_op jit(solution)/shard_map/ppermute | solution.py:62
  461.9 6.8 %copy-start.1 = (f32[2048,32]{0,1:T(8,128)}, f32[2048,32]{0,1:T(8,128)S(1)}, u32[]{:S(2)}) copy-start(f32[2048,32]{0,1:T(8,128)S(1)} %add_bitcast_fusion) | copy-start | bytes 786436
Sparse Core Ops, SparseCore 0:
  10.8 21.9 reduce-scatter.21
  35.1 25.4 reduce-scatter.15
  63.7 52.3 all-reduce.3
  154.9 15.9 reduce-scatter.23
  173.0 25.4 reduce-scatter.17
  201.4 52.3 all-reduce.5
  293.7 15.9 reduce-scatter.25
  311.9 25.3 reduce-scatter.19
  340.4 52.3 all-reduce.7
  432.5 15.8 reduce-scatter.27
